TPU v7x, 512 devices: a whole 4x4x16 slice. The times are simulated.
512 devices in a mesh: lvl: 4 (over z_lo), gx: 16 (over y, z_hi), gy: 8 (over x, core).
Axes of the slice: x: 4, y: 4, z: 16 (z_hi: 4, z_lo: 4; z = z_hi * 4 + z_lo), core: 2. Of those that a mesh axis runs over, the one named last changes fastest.
Arguments:
- initial: float32 [256, 256, 256], P('gx', 'gy'), may hold values from -6 to 6
- reaction: float32 [256, 256, 256], P('gx', 'gy'), may hold values from -0.5 to 0
Outputs:
- levels: float32 [4, 256, 256, 256], P('lvl', 'gx', 'gy')
All inputs are finite; a program needn't handle non-finite values.
Results may differ from a plain program's by a relative error of at most 0.0001.
Values sent between devices are 32-bit elements; how exact they have to be, the bound alone decides.
A program may use at most 64 MiB of HBM per device.

v0:
```python
import math

import jax
import jax.numpy as jnp
from jax import lax
from jax.sharding import PartitionSpec as P

STEPS = 1


DIFFUSE = 0.3
HIGHEST = lax.Precision.HIGHEST


def phases_at(points, length, count, first):
    wavenum = lax.broadcasted_iota(jnp.int32, (points.shape[0], count), 1) + first
    turns = points[:, None] * wavenum % length
    angles = turns.astype(jnp.float32) * (2.0 * math.pi / length)
    return (jnp.cos(angles), jnp.sin(angles))


def phases(length, count, first):
    points = lax.broadcasted_iota(jnp.int32, (length,), 0)
    return phases_at(points, length, count, first)


def table_from(cosine, sine, direction):
    turned = direction * sine
    return jnp.stack([jnp.stack([cosine, turned], axis=1), jnp.stack([-turned, cosine], axis=1)])


def spectral_factor(first_x, count_x, first_y, count_y, first_z, count_z, scales, norm):
    wave_z = (lax.broadcasted_iota(jnp.int32, (count_z, 1, 1), 0) + first_z).astype(
        jnp.float32
    ) / scales[2]
    wave_x = (lax.broadcasted_iota(jnp.int32, (1, count_x, 1), 1) + first_x).astype(
        jnp.float32
    ) / scales[0]
    wave_y = (lax.broadcasted_iota(jnp.int32, (1, 1, count_y), 2) + first_y).astype(
        jnp.float32
    ) / scales[1]
    factor_real = -DIFFUSE * (wave_x * wave_x + wave_y * wave_y + wave_z * wave_z) * norm
    factor_imag = -(0.3 * wave_x + 0.2 * wave_y + 0.25 * wave_z) * norm
    return (factor_real, factor_imag)


def shards(initial, reaction):
    rows_x, rows_y, depth = initial.shape
    parts_x = lax.axis_size("gx")
    parts_y = lax.axis_size("gy")
    level_count = lax.axis_size("lvl")
    full_x = rows_x * parts_x
    full_y = rows_y * parts_y
    modes_x = full_x // 2
    modes_y = full_y // 2
    modes_z = depth // 4
    scales = (full_x // 4, full_y // 4, depth // 4)
    norm = 1.0 / (full_x * full_y * depth)
    cosine_z, sine_z = phases(depth, modes_z, 0)
    forward_table = jnp.stack([cosine_z, -sine_z], axis=2)
    weights = jnp.where(lax.broadcasted_iota(jnp.int32, (1, modes_z), 1) == 0, 1.0, 2.0).astype(
        jnp.float32
    )
    back_z = jnp.stack([(cosine_z * weights).T, -(sine_z * weights).T], axis=1)
    cosine_y, sine_y = phases(full_y, modes_y, -(modes_y // 2))
    forward_y = table_from(cosine_y, sine_y, -1.0)
    back_y = table_from(cosine_y.T, sine_y.T, 1.0)
    block_x = modes_x // parts_y
    level_index = lax.axis_index("lvl")

    def make_rate(points, parts, joint_index, react):
        block_z = modes_z // parts
        cosine_x, sine_x = phases_at(points, full_x, modes_x, -(modes_x // 2))
        forward_x = table_from(cosine_x, sine_x, -1.0)
        back_x = table_from(cosine_x.T, sine_x.T, 1.0)
        z_back = back_z.reshape(parts, block_z, 2, depth)
        factor_real, factor_imag = spectral_factor(
            lax.axis_index("gy") * block_x - modes_x // 2,
            block_x,
            -(modes_y // 2),
            modes_y,
            joint_index * block_z,
            block_z,
            scales,
            norm,
        )

        def x_lines(block_data):
            return jnp.einsum("abpyx,pxqk->abqky", block_data, forward_x, precision=HIGHEST)

        def z_lines(block_data):
            return jnp.einsum("abpyx,abpz->xyz", block_data, z_back, precision=HIGHEST)

        def rate(grid_field):
            spectrum = jnp.einsum("xyz,zkp->kpyx", grid_field, forward_table, precision=HIGHEST)
            spectrum = spectrum.reshape(parts, block_z, 2, grid_field.shape[1], grid_field.shape[0])
            wide_form = x_lines(
                lax.all_to_all(spectrum, ("lvl", "gx"), split_axis=0, concat_axis=4, tiled=True)
            )
            tall_form = lax.all_to_all(wide_form, "gy", split_axis=3, concat_axis=4, tiled=True)
            tall_form = jnp.einsum("abpxy,pyqk->abqxk", tall_form, forward_y, precision=HIGHEST)
            real_part = tall_form[:, :, 0]
            imag_part = tall_form[:, :, 1]
            tall_form = jnp.stack(
                [
                    factor_real * real_part - factor_imag * imag_part,
                    factor_real * imag_part + factor_imag * real_part,
                ],
                axis=2,
            )
            tall_form = jnp.einsum("abpxk,pkqy->abqxy", tall_form, back_y, precision=HIGHEST)
            wide_form = lax.all_to_all(tall_form, "gy", split_axis=4, concat_axis=3, tiled=True)
            wide_form = jnp.einsum("abpky,pkqx->abqyx", wide_form, back_x, precision=HIGHEST)
            values = z_lines(
                lax.all_to_all(wide_form, ("lvl", "gx"), split_axis=4, concat_axis=0, tiled=True)
            )
            return values + react * grid_field

        return rate

    slab_rows = rows_x // level_count
    joint_parts = parts_x * level_count
    places = lax.broadcasted_iota(jnp.int32, (full_x,), 0)
    source = places // slab_rows
    points = source % parts_x * rows_x + source // parts_x * slab_rows + places % slab_rows
    joint_index = level_index * parts_x + lax.axis_index("gx")
    start = level_index * slab_rows
    own_initial = lax.dynamic_slice_in_dim(initial, start, slab_rows, 0)
    own_reaction = lax.dynamic_slice_in_dim(reaction, start, slab_rows, 0)
    slab_rate = make_rate(points, joint_parts, joint_index, own_reaction)
    start_rate = slab_rate(own_initial)
    earlier = None
    finals = []
    for level_number in range(level_count):
        current = own_initial
        rates = [start_rate]
        update = current + rates[0]
        if earlier is not None:
            update = update + 0.5 * (earlier[1] - earlier[0])
        current = update
        if level_number < level_count - 1 or 0 < STEPS - 1:
            rates.append(slab_rate(current))
        finals.append(current)
        earlier = rates
    stacked = jnp.stack(finals)
    return lax.all_to_all(stacked, "lvl", split_axis=0, concat_axis=1, tiled=True)


def solution(mesh):
    in_specs = (P("gx", "gy", None), P("gx", "gy", None))
    out_specs = P("lvl", "gx", "gy", None)
    return jax.shard_map(shards, mesh=mesh, in_specs=in_specs, out_specs=out_specs, check_vma=False)
```

profile of v0, /device:TPU:1, one launch (start us, length us, event | category | flops | bytes accessed | tf_op | source)
XLA Modules:
  0.0 295.6 jit_solution(5902834742624659790)
XLA Ops:
  0.3 1.3 convolution_bitcast_fusion.7
  2.5 19.3 %all-to-all-start = ((f32[64,1,256]{2,1,0:T(1,128)}), f32[64,1,256]{2,1,0:T(1,128)S(1)}, u32[]{:S(2)}, u32[]{:S(2)}) async-start(f32[64,1,256]{2,1,0:T(1,128)} %reshape.1420), calls=%async_computation | async-start | bytes 131072 | tf_op jit(solution)/shard_map/all_to_all | solution.py:98
  24.2 11.3 %all-to-all-done = f32[64,1,256]{2,1,0:T(1,128)S(1)} async-done(((f32[64,1,256]{2,1,0:T(1,128)}), f32[64,1,256]{2,1,0:T(1,128)S(1)}, u32[]{:S(2)}, u32[]{:S(2)}) %all-to-all-start) | async-done | bytes 65568 | tf_op jit(solution)/shard_map/all_to_all | solution.py:98
  38.7 6.6 %all-to-all-start.1 = ((f32[8,1,1024]{2,1,0:T(1,128)}), f32[8,1,1024]{2,1,0:T(1,128)S(1)}, u32[]{:S(2)}, u32[]{:S(2)}) async-start(f32[8,1,1024]{2,1,0:T(1,128)} %reshape.1422), calls=%async_computation.1 | async-start | bytes 65536 | tf_op jit(solution)/shard_map/all_to_all | solution.py:100
  45.2 4.7 %all-to-all-done.1 = f32[8,1,1024]{2,1,0:T(1,128)S(1)} async-done(((f32[8,1,1024]{2,1,0:T(1,128)}), f32[8,1,1024]{2,1,0:T(1,128)S(1)}, u32[]{:S(2)}, u32[]{:S(2)}) %all-to-all-start.1) | async-done | bytes 32800 | tf_op jit(solution)/shard_map/all_to_all | solution.py:100
  53.0 4.0 %all-to-all-start.2 = ((f32[8,1,1024]{2,1,0:T(1,128)}), f32[8,1,1024]{2,1,0:T(1,128)S(1)}, u32[]{:S(2)}, u32[]{:S(2)}) async-start(f32[8,1,1024]{2,1,0:T(1,128)} %reshape.1424), calls=%async_computation.2 | async-start | bytes 65536 | tf_op jit(solution)/shard_map/all_to_all | solution.py:112
  57.0 4.7 %all-to-all-done.2 = f32[8,1,1024]{2,1,0:T(1,128)S(1)} async-done(((f32[8,1,1024]{2,1,0:T(1,128)}), f32[8,1,1024]{2,1,0:T(1,128)S(1)}, u32[]{:S(2)}, u32[]{:S(2)}) %all-to-all-start.2) | async-done | bytes 32800 | tf_op jit(solution)/shard_map/all_to_all | solution.py:112
  64.5 4.6 %all-to-all-start.3 = ((f32[64,1,256]{2,1,0:T(1,128)}), f32[64,1,256]{2,1,0:T(1,128)S(1)}, u32[]{:S(2)}, u32[]{:S(2)}) async-start(f32[64,1,256]{2,1,0:T(1,128)} %reshape.1426), calls=%async_computation.3 | async-start | bytes 131072 | tf_op jit(solution)/shard_map/all_to_all | solution.py:115
  69.4 13.2 %all-to-all-done.3 = f32[64,1,256]{2,1,0:T(1,128)S(1)} async-done(((f32[64,1,256]{2,1,0:T(1,128)}), f32[64,1,256]{2,1,0:T(1,128)S(1)}, u32[]{:S(2)}, u32[]{:S(2)}) %all-to-all-start.3) | async-done | bytes 65568 | tf_op jit(solution)/shard_map/all_to_all | solution.py:115
  85.9 18.4 %all_to_all.252 = f32[64,1,256]{2,1,0:T(1,128)S(1)} all-to-all(f32[64,1,256]{2,1,0:T(1,128)S(1)} %reshape.1428), channel_id=1, replica_groups=mesh['lvl'=4,'gx'=16,'gy'=8] {'lvl','gx'}, dimensions={0} | all-to-all | bytes 131072 | tf_op jit(solution)/shard_map/all_to_all | solution.py:98
  106.3 9.6 %all_to_all.253 = f32[8,1,1024]{2,1,0:T(1,128)S(1)} all-to-all(f32[8,1,1024]{2,1,0:T(1,128)S(1)} %reshape.1430), channel_id=1, replica_groups=mesh['lvl'=4,'gx'=16,'gy'=8] {'gy'}, dimensions={0} | all-to-all | bytes 65536 | tf_op jit(solution)/shard_map/all_to_all | solution.py:100
  118.3 7.8 %all_to_all.254 = f32[8,1,1024]{2,1,0:T(1,128)S(1)} all-to-all(f32[8,1,1024]{2,1,0:T(1,128)S(1)} %reshape.1432), channel_id=1, replica_groups=mesh['lvl'=4,'gx'=16,'gy'=8] {'gy'}, dimensions={0} | all-to-all | bytes 65536 | tf_op jit(solution)/shard_map/all_to_all | solution.py:112
  128.3 17.4 %all_to_all.255 = f32[64,1,256]{2,1,0:T(1,128)S(1)} all-to-all(f32[64,1,256]{2,1,0:T(1,128)S(1)} %reshape.1434), channel_id=1, replica_groups=mesh['lvl'=4,'gx'=16,'gy'=8] {'lvl','gx'}, dimensions={0} | all-to-all | bytes 131072 | tf_op jit(solution)/shard_map/all_to_all | solution.py:115
  146.9 1.2 fusion.12
  148.8 17.7 %all_to_all.256 = f32[64,1,256]{2,1,0:T(1,128)S(1)} all-to-all(f32[64,1,256]{2,1,0:T(1,128)S(1)} %reshape.1436), channel_id=1, replica_groups=mesh['lvl'=4,'gx'=16,'gy'=8] {'lvl','gx'}, dimensions={0} | all-to-all | bytes 131072 | tf_op jit(solution)/shard_map/all_to_all | solution.py:98
  168.6 10.4 %all_to_all.257 = f32[8,1,1024]{2,1,0:T(1,128)S(1)} all-to-all(f32[8,1,1024]{2,1,0:T(1,128)S(1)} %reshape.1438), channel_id=1, replica_groups=mesh['lvl'=4,'gx'=16,'gy'=8] {'gy'}, dimensions={0} | all-to-all | bytes 65536 | tf_op jit(solution)/shard_map/all_to_all | solution.py:100
  181.4 7.8 %all_to_all.258 = f32[8,1,1024]{2,1,0:T(1,128)S(1)} all-to-all(f32[8,1,1024]{2,1,0:T(1,128)S(1)} %reshape.1440), channel_id=1, replica_groups=mesh['lvl'=4,'gx'=16,'gy'=8] {'gy'}, dimensions={0} | all-to-all | bytes 65536 | tf_op jit(solution)/shard_map/all_to_all | solution.py:112
  192.9 17.4 %all_to_all.259 = f32[64,1,256]{2,1,0:T(1,128)S(1)} all-to-all(f32[64,1,256]{2,1,0:T(1,128)S(1)} %reshape.1442), channel_id=1, replica_groups=mesh['lvl'=4,'gx'=16,'gy'=8] {'lvl','gx'}, dimensions={0} | all-to-all | bytes 131072 | tf_op jit(solution)/shard_map/all_to_all | solution.py:115
  215.0 17.8 %all_to_all.260 = f32[64,1,256]{2,1,0:T(1,128)S(1)} all-to-all(f32[64,1,256]{2,1,0:T(1,128)S(1)} %reshape.1444), channel_id=1, replica_groups=mesh['lvl'=4,'gx'=16,'gy'=8] {'lvl','gx'}, dimensions={0} | all-to-all | bytes 131072 | tf_op jit(solution)/shard_map/all_to_all | solution.py:98
  234.8 10.2 %all_to_all.261 = f32[8,1,1024]{2,1,0:T(1,128)S(1)} all-to-all(f32[8,1,1024]{2,1,0:T(1,128)S(1)} %reshape.1446), channel_id=1, replica_groups=mesh['lvl'=4,'gx'=16,'gy'=8] {'gy'}, dimensions={0} | all-to-all | bytes 65536 | tf_op jit(solution)/shard_map/all_to_all | solution.py:100
  247.4 7.8 %all_to_all.262 = f32[8,1,1024]{2,1,0:T(1,128)S(1)} all-to-all(f32[8,1,1024]{2,1,0:T(1,128)S(1)} %reshape.1448), channel_id=1, replica_groups=mesh['lvl'=4,'gx'=16,'gy'=8] {'gy'}, dimensions={0} | all-to-all | bytes 65536 | tf_op jit(solution)/shard_map/all_to_all | solution.py:112
  258.0 4.6 %all-to-all-start.15 = ((f32[64,1,256]{2,1,0:T(1,128)}), f32[64,1,256]{2,1,0:T(1,128)S(1)}, u32[]{:S(2)}, u32[]{:S(2)}) async-start(f32[64,1,256]{2,1,0:T(1,128)} %reshape.1450), calls=%async_computation.15 | async-start | bytes 131072 | tf_op jit(solution)/shard_map/all_to_all | solution.py:115
  262.7 13.5 %all-to-all-done.15 = f32[64,1,256]{2,1,0:T(1,128)S(1)} async-done(((f32[64,1,256]{2,1,0:T(1,128)}), f32[64,1,256]{2,1,0:T(1,128)S(1)}, u32[]{:S(2)}, u32[]{:S(2)}) %all-to-all-start.15) | async-done | bytes 65568 | tf_op jit(solution)/shard_map/all_to_all | solution.py:115
  278.7 16.1 %all_to_all.263 = f32[4,4,32,256]{3,2,1,0:T(8,128)S(1)} all-to-all(f32[4,4,32,256]{3,2,1,0:T(8,128)S(1)} %pad_maximum_fusion.4), channel_id=1, replica_groups=mesh['lvl'=4,'gx'=16,'gy'=8] {'lvl'}, dimensions={0} | all-to-all | bytes 1048576 | tf_op jit(solution)/shard_map/all_to_all | solution.py:146
  (137 shorter events, 47.3 us)
Async XLA Ops:
  2.5 33.0 %all-to-all-start = ((f32[64,1,256]{2,1,0:T(1,128)}), f32[64,1,256]{2,1,0:T(1,128)S(1)}, u32[]{:S(2)}, u32[]{:S(2)}) async-start(f32[64,1,256]{2,1,0:T(1,128)} %reshape.1420), calls=%async_computation | async-start | bytes 131072 | tf_op jit(solution)/shard_map/all_to_all | solution.py:98
  38.7 11.3 %all-to-all-start.1 = ((f32[8,1,1024]{2,1,0:T(1,128)}), f32[8,1,1024]{2,1,0:T(1,128)S(1)}, u32[]{:S(2)}, u32[]{:S(2)}) async-start(f32[8,1,1024]{2,1,0:T(1,128)} %reshape.1422), calls=%async_computation.1 | async-start | bytes 65536 | tf_op jit(solution)/shard_map/all_to_all | solution.py:100
  53.0 8.7 %all-to-all-start.2 = ((f32[8,1,1024]{2,1,0:T(1,128)}), f32[8,1,1024]{2,1,0:T(1,128)S(1)}, u32[]{:S(2)}, u32[]{:S(2)}) async-start(f32[8,1,1024]{2,1,0:T(1,128)} %reshape.1424), calls=%async_computation.2 | async-start | bytes 65536 | tf_op jit(solution)/shard_map/all_to_all | solution.py:112
  64.5 18.2 %all-to-all-start.3 = ((f32[64,1,256]{2,1,0:T(1,128)}), f32[64,1,256]{2,1,0:T(1,128)S(1)}, u32[]{:S(2)}, u32[]{:S(2)}) async-start(f32[64,1,256]{2,1,0:T(1,128)} %reshape.1426), calls=%async_computation.3 | async-start | bytes 131072 | tf_op jit(solution)/shard_map/all_to_all | solution.py:115
  69.1 14.8 %copy-start = (f32[16,32,256]{2,1,0:T(8,128)S(1)}, f32[16,32,256]{2,1,0:T(8,128)}, u32[]{:S(2)}) copy-start(f32[16,32,256]{2,1,0:T(8,128)} %param.2) | copy-start | bytes 1572868
  258.0 18.2 %all-to-all-start.15 = ((f32[64,1,256]{2,1,0:T(1,128)}), f32[64,1,256]{2,1,0:T(1,128)S(1)}, u32[]{:S(2)}, u32[]{:S(2)}) async-start(f32[64,1,256]{2,1,0:T(1,128)} %reshape.1450), calls=%async_computation.15 | async-start | bytes 131072 | tf_op jit(solution)/shard_map/all_to_all | solution.py:115
where the time goes:
time: 297 us; the launch traced here: 296 us
  blocking collectives  158 us (53%)
  waiting for transfers between devices  47.5 us (16%)
  starting transfers between devices  39 us (13%)
  local copies, waits for them, and re-layouts  18.1 us (6%)
  other arithmetic  16.2 us (5%)
  matrix products  15.6 us (5%)
    all_to_all x3, blocking collectives, rate(): lax.all_to_all(spectrum, ('lvl', 'gx'), split_axis=0, concat_axis=4, tile...  53.9 us
    all_to_all x2, blocking collectives, rate(): lax.all_to_all(wide_form, ('lvl', 'gx'), split_axis=4, concat_axis=0, til...  34.8 us
    all_to_all x3, blocking collectives, rate(): lax.all_to_all(wide_form, 'gy', split_axis=3, concat_axis=4, tiled=True)  30.2 us
    all_to_all x2, waiting for transfers between devices, rate(): lax.all_to_all(wide_form, ('lvl', 'gx'), split_axis=4, concat_axis=0, til...  26.8 us
    all_to_all x3, blocking collectives, rate(): lax.all_to_all(tall_form, 'gy', split_axis=4, concat_axis=3, tiled=True)  23.4 us
    all_to_all x1, starting transfers between devices, rate(): lax.all_to_all(spectrum, ('lvl', 'gx'), split_axis=0, concat_axis=4, tile...  19.3 us
    all_to_all x1, blocking collectives, shards(): lax.all_to_all(stacked, 'lvl', split_axis=0, concat_axis=1, tiled=True)  16.1 us
    unnamed x35, local copies, waits for them, and re-layouts  11.5 us
  transfers between devices with their start and end apart: 5, of which 5 were waited for; matrix products, arithmetic and copies ran while one was open for 1% of the time, Pallas kernels for 0%

commit v1 on v0

v1 whole, which is shorter than its diff:
```python
import functools
import math

import jax
import jax.numpy as jnp
import numpy as np
from jax import lax
from jax.experimental import pallas as pl
from jax.experimental.pallas import tpu as pltpu
from jax.sharding import PartitionSpec as P

CELLS = 256
MODES = 128
DEPTH_MODES = 64
LEVELS = 4
PARTS_X = 16
PARTS_Y = 8
PLANE = LEVELS * PARTS_X
SLAB = CELLS // PLANE
ROWS_Y = CELLS // PARTS_Y
ROWS_X = CELLS // PARTS_X
RING_Z = 16
RING_Y = 4
DIFFUSE = 0.3
NORM = 1.0 / CELLS**3
LANES = 128
MESH = pl.DeviceIdType.MESH
F32 = jnp.float32
BF16 = jnp.bfloat16

Y_OUT, X_OUT, X_BACK, Y_BACK, Y_OUT2, X_OUT2, X_BACK2, BULK, FINAL = range(9)
PHASES = FINAL + LEVELS


def halves(table):
    high = table.astype(BF16)
    low = (table - high.astype(np.float64)).astype(BF16)
    return np.concatenate([high, low], axis=0)


def tables():
    points = np.arange(CELLS)
    step = 2.0 * math.pi / CELLS

    def phase(wave):
        angle = (points[:, None] * wave[None, :] % CELLS) * step
        return np.cos(angle), np.sin(angle)

    wave_z = np.arange(DEPTH_MODES)
    cos_z, sin_z = phase(wave_z)
    per_part = DEPTH_MODES // PARTS_Y

    def parts(real, imag):
        stacked = np.stack([real, imag], axis=1)
        stacked = stacked.reshape(CELLS, 2, PARTS_Y, per_part)
        return stacked.transpose(0, 2, 1, 3).reshape(CELLS, LANES)

    forward_z = parts(cos_z, -sin_z)
    weight = np.where(wave_z == 0, 1.0, 2.0)
    back_z = parts(cos_z * weight, -sin_z * weight).T

    wave = np.arange(MODES) - MODES // 2
    cosine, sine = phase(wave)
    forward_y = np.concatenate([cosine.T, sine.T], axis=0)
    back_y = np.concatenate([cosine, sine], axis=1)
    order = (np.arange(PLANE)[None, :] * SLAB + np.arange(SLAB)[:, None]).reshape(-1)
    forward_x = forward_y[:, order]
    back_x = back_y[order, :]
    return [halves(t) for t in (forward_z, forward_y, forward_x, back_x, back_y, back_z)]


def split(x):
    high = x.astype(BF16)
    return high, (x - high.astype(F32)).astype(BF16)


def dot(a, b):
    return jnp.dot(a, b, preferred_element_type=F32)


def table_times(table, data):
    rows = table.shape[0] // 2
    high, low = split(data)
    first = dot(table[...], high)
    return first[:rows] + first[rows:] + dot(table[:rows, :], low)


def times_table(data, table):
    depth = table.shape[0] // 2
    rows = data.shape[0]
    high, low = split(data)
    first = dot(jnp.concatenate([high, low], axis=0), table[:depth, :])
    return first[:rows] + first[rows:] + dot(high, table[depth:, :])


def lane_index(shape):
    return lax.broadcasted_iota(jnp.int32, shape, 1)


def roll(x, shift):
    return x if shift % LANES == 0 else pltpu.roll(x, shift % LANES, 1)


def turn(x):
    real = (lane_index(x.shape) & 8) == 0
    return jnp.where(real, -roll(x, -8), roll(x, 8))


def swap_groups(mats):
    mats = list(mats)
    group = lane_index(mats[0].shape) // 16
    for bit in (1, 2, 4):
        keep = (group & bit) == 0
        for low in range(8):
            if low & bit:
                continue
            high = low | bit
            a, b = mats[low], mats[high]
            mats[low] = jnp.where(keep, a, roll(b, 16 * bit))
            mats[high] = jnp.where(keep, roll(a, -16 * bit), b)
    return mats


def kernel(
    v_hbm, r_hbm, tz_hbm, ty_hbm, tx_hbm, bx_hbm, by_hbm, bz_hbm, out_hbm,
    v, r, r_all, tz, ty, tx, bx, by, bz,
    factor, carry, y_send, y_recv, x_send, x_recv, b_send, b_recv, u_send, u_recv, f_recv,
    piece_send, piece, load_sem, send_sem, recv_sem,
):
    lvl, gx, gy = lax.axis_index("lvl"), lax.axis_index("gx"), lax.axis_index("gy")
    row_y, high_z = lax.div(gx, 4), lax.rem(gx, 4)
    at_z = high_z * 4 + lvl
    me = row_y * RING_Z + at_z

    def plane_id(y2, z2):
        return {"gx": y2 * 4 + lax.div(z2, 4), "lvl": lax.rem(z2, 4)}

    def over_plane(do):
        def body(k, carried):
            half = lax.div(k + 1, 2)
            dz = 8 + half * (1 - 2 * lax.rem(k, 2))
            z2 = lax.rem(at_z + dz, RING_Z)
            for dy in (2, 1, 3, 0):
                do(lax.rem(row_y + dy, RING_Y), z2)
            return carried

        lax.fori_loop(0, RING_Z - 1, body, 0)
        for dy in (2, 1, 3):
            do(lax.rem(row_y + dy, RING_Y), at_z)

    barrier = pltpu.get_barrier_semaphore()

    def hello(y2, z2):
        pl.semaphore_signal(barrier, inc=1, device_id=plane_id(y2, z2), device_id_type=MESH)

    over_plane(hello)
    for k in range(1, PARTS_Y):
        pl.semaphore_signal(
            barrier, inc=1, device_id={"gy": lax.rem(gy + k, PARTS_Y)}, device_id_type=MESH
        )

    own = pl.ds(lvl * SLAB, SLAB)
    loads = [
        pltpu.make_async_copy(source, target, load_sem.at[i])
        for i, (source, target) in enumerate(
            [
                (v_hbm.at[own], v),
                (r_hbm.at[own], r),
                (tz_hbm, tz),
                (ty_hbm, ty),
                (tx_hbm, tx),
                (bx_hbm, bx),
                (by_hbm, by),
                (bz_hbm, bz),
                (r_hbm, r_all),
            ]
        )
    ]
    for load in loads:
        load.start()

    def remote(source, target, phase, device_id, send_phase=None):
        return pltpu.make_async_remote_copy(
            src_ref=source,
            dst_ref=target,
            send_sem=send_sem.at[phase if send_phase is None else send_phase],
            recv_sem=recv_sem.at[phase],
            device_id=device_id,
            device_id_type=MESH,
        )

    def received(ref, phase):
        remote(ref, ref, phase, {"gy": gy}).wait_recv()

    def sent(ref, phase):
        remote(ref, ref, phase, {"gy": gy}).wait_send()

    def y_exchange(source, target, phase):
        for k in (4, 3, 5, 2, 6, 1, 7):
            other = lax.rem(gy + k, PARTS_Y)
            remote(source.at[other], target.at[gy], phase, {"gy": other}).start()
        target[gy] = source[gy]

    def x_exchange(source, target, phase, shift):
        def chunk_of(y2, z2):
            return y2 * RING_Z + lax.rem(z2 + RING_Z - shift, RING_Z)

        def send(y2, z2):
            remote(source.at[chunk_of(y2, z2)], target.at[me], phase, plane_id(y2, z2)).start()

        over_plane(send)
        target[me] = source[chunk_of(row_y, at_z)]

    shape = (MODES, LANES)
    lane = lane_index(shape)
    wave_x = (lax.broadcasted_iota(jnp.int32, shape, 0) - MODES // 2).astype(F32) / (CELLS // 4)
    wave_y = ((lane // 32 & 1) + 2 * me - MODES // 2).astype(F32) / (CELLS // 4)
    wave_z = ((lane & 7) + 8 * gy).astype(F32) / (CELLS // 4)
    factor[0] = -DIFFUSE * (wave_x * wave_x + wave_y * wave_y + wave_z * wave_z) * NORM
    factor[1] = -(0.3 * wave_x + 0.2 * wave_y + 0.25 * wave_z) * NORM
    edge = (wave_z == 0.0) & ((wave_x == -1.0) | (wave_y == -1.0))
    factor[2] = jnp.where(edge, 0.5 / NORM, 1.0 / NORM)

    def scaled(x):
        return factor[0] * x + factor[1] * turn(x)

    def z_forward(first, second):
        lines = times_table(jnp.concatenate([first, second], axis=0), tz)
        mats = [
            lines[(field * SLAB + i) * ROWS_Y : (field * SLAB + i + 1) * ROWS_Y]
            for i in range(SLAB)
            for field in range(2)
        ]
        for part, mat in enumerate(swap_groups(mats)):
            y_send[part] = mat

    def z_back(mats):
        lines = swap_groups(mats)
        stacked = jnp.concatenate([lines[2 * i + f] for f in range(2) for i in range(SLAB)], axis=0)
        values = times_table(stacked, bz)
        half = SLAB * ROWS_Y
        return values[:half], values[half:]

    def y_forward():
        both = table_times(ty, y_recv[...].reshape(CELLS, LANES))
        lines = both[:MODES] - turn(both[MODES:])
        x_send.reshape(MODES, LANES)[...] = lines

    def x_middle(carried):
        rows = x_recv.reshape(MODES, LANES)
        first = rows[pl.ds(0, PLANE, stride=2), :]
        second = rows[pl.ds(1, PLANE, stride=2), :]
        low = lane_index(first.shape) < 32
        lines = jnp.concatenate(
            [
                jnp.where(low, roll(first, -32 * i), roll(second, 32 - 32 * i))
                for i in range(SLAB)
            ],
            axis=0,
        )
        both = table_times(tx, lines)
        spectrum = both[:MODES] - turn(both[MODES:])
        is_first = (lane & 16) == 0
        if carried:
            spectrum = spectrum + jnp.where(is_first, roll(factor[2] * carry[...], -16), 0.0)
        rate = scaled(spectrum)
        rate = jnp.where(is_first, rate, scaled(roll(factor[2] * rate, 16) + spectrum))
        if not carried:
            carry[...] = rate
        lines = table_times(bx, jnp.concatenate([rate, turn(rate)], axis=0))
        group = lane_index((PLANE, LANES)) // 32
        target = b_send.reshape(MODES, LANES)
        for ky in range(2):
            out = None
            for i in range(SLAB):
                piece_i = roll(lines[i * PLANE : (i + 1) * PLANE], 32 * (i - ky))
                out = piece_i if out is None else jnp.where(group == i, piece_i, out)
            target[pl.ds(ky, PLANE, stride=2), :] = out

    def y_back():
        lines = b_recv.reshape(MODES, LANES)[...]
        cells = table_times(by, jnp.concatenate([lines, turn(lines)], axis=0))
        u_send[...] = cells.reshape(PARTS_Y, ROWS_Y, LANES)

    for i in range(3):
        loads[i].wait()
    start = v[...].reshape(SLAB * ROWS_Y, CELLS)
    react = r[...].reshape(SLAB * ROWS_Y, CELLS)
    z_forward(start, react * start)
    for i in range(3, 8):
        loads[i].wait()
    pl.semaphore_wait(barrier, PLANE - 1 + PARTS_Y - 1)

    others_y = pl.ds(0, PARTS_Y - 1)
    others_x = pl.ds(0, PLANE - 1)
    y_exchange(y_send, y_recv, Y_OUT)
    received(y_recv.at[others_y], Y_OUT)
    y_forward()
    x_exchange(x_send, x_recv, X_OUT, 0)
    received(x_recv.at[others_x], X_OUT)
    x_middle(False)
    x_exchange(b_send, b_recv, X_BACK, 0)
    received(b_recv.at[others_x], X_BACK)
    y_back()
    sent(y_send.at[others_y], Y_OUT)
    y_exchange(u_send, u_recv, Y_BACK)
    received(u_recv.at[others_y], Y_BACK)
    smooth, smooth_rate = z_back([u_recv[part] for part in range(PARTS_Y)])
    rate1 = smooth + react * start
    rate2 = smooth_rate + react * rate1
    z_forward(react * rate1, react * rate2)

    sent(x_send.at[others_x], X_OUT)
    sent(b_send.at[others_x], X_BACK)
    y_exchange(y_send, y_recv, Y_OUT2)
    known = start + rate1
    piece_send[0] = known.reshape(SLAB, ROWS_Y, CELLS)
    known = known + 0.5 * rate2
    piece_send[1] = known.reshape(SLAB, ROWS_Y, CELLS)
    known = known + 0.25 * (react * rate2)
    piece_send[2] = known.reshape(SLAB, ROWS_Y, CELLS)
    known = known + 0.125 * (react * (react * rate2))
    piece_send[3] = known.reshape(SLAB, ROWS_Y, CELLS)
    for k in range(1, LEVELS):
        other = lax.rem(lvl + k, LEVELS)
        remote(piece_send.at[other], piece.at[own], BULK, {"lvl": other}).start()
    piece[own] = piece_send[lvl]

    received(y_recv.at[others_y], Y_OUT2)
    y_forward()
    x_exchange(x_send, x_recv, X_OUT2, 0)
    received(x_recv.at[others_x], X_OUT2)
    x_middle(True)
    x_exchange(b_send, b_recv, X_BACK2, 1)
    received(b_recv.at[others_x], X_BACK2)
    sent(u_send.at[others_y], Y_BACK)
    y_back()

    before = lax.rem(at_z + RING_Z - 1, RING_Z)
    slab, block = lax.rem(before, 4), row_y * 4 + lax.div(before, 4)

    def last(level, k):
        other = lax.rem(gy + k, PARTS_Y)
        remote(
            u_send.at[other],
            f_recv.at[slab, gy],
            FINAL + slab,
            {"lvl": level, "gx": block, "gy": other},
            FINAL + level,
        ).start()

    for k in (4, 3, 5, 2, 6, 1, 7):
        for level in (3, 2):
            last(level, k)
    for level in (3, 2):
        @pl.when(lvl != level)
        def _(level=level):
            last(level, 0)

        @pl.when(lvl == level)
        def _():
            f_recv[slab, gy] = u_send[gy]

    loads[8].wait()
    received(piece.at[pl.ds(0, ROWS_X - SLAB)], BULK)

    @pl.when(lvl >= 2)
    def _():
        last_weight = jnp.where(lvl == 3, 0.125, 0.0)
        for t in range(LEVELS):
            @pl.when(lvl - 1 != t)
            def _(t=t):
                received(f_recv.at[t], FINAL + t)

            @pl.when(lvl - 1 == t)
            def _(t=t):
                received(f_recv.at[t, others_y], FINAL + t)

            first, second = z_back([f_recv[t, part] for part in range(PARTS_Y)])
            at = pl.ds(t * SLAB, SLAB)
            first = first.reshape(SLAB, ROWS_Y, CELLS)
            second = second.reshape(SLAB, ROWS_Y, CELLS)
            piece[at] = piece[at] + (0.25 + last_weight * r_all[at]) * first + last_weight * second

    result = pltpu.make_async_copy(piece, out_hbm.at[0], load_sem.at[0])
    result.start()

    sent(y_send.at[others_y], Y_OUT2)
    sent(x_send.at[others_x], X_OUT2)
    sent(b_send.at[others_x], X_BACK2)
    sent(piece_send.at[pl.ds(0, 3)], BULK)
    for level in (3, 2):
        @pl.when(lvl != level)
        def _(level=level):
            sent(u_send, FINAL + level)

        @pl.when(lvl == level)
        def _(level=level):
            sent(u_send.at[others_y], FINAL + level)

    result.wait()


def solution(mesh):
    constants = tables()

    def shards(initial, reaction):
        rows = (SLAB, ROWS_Y, CELLS)
        block = (ROWS_X, ROWS_Y, CELLS)
        lines = (PARTS_Y, ROWS_Y, LANES)
        chunks = (PLANE, 2, LANES)
        vmem = pltpu.VMEM
        return pl.pallas_call(
            kernel,
            out_shape=jax.ShapeDtypeStruct((1, *block), F32),
            in_specs=[pl.BlockSpec(memory_space=pl.ANY)] * 8,
            out_specs=pl.BlockSpec(memory_space=pl.ANY),
            scratch_shapes=[
                vmem(rows, F32),
                vmem(rows, F32),
                vmem(block, F32),
                *[vmem(t.shape, BF16) for t in constants],
                vmem((3, MODES, LANES), F32),
                vmem((MODES, LANES), F32),
                vmem(lines, F32),
                vmem(lines, F32),
                vmem(chunks, F32),
                vmem(chunks, F32),
                vmem(chunks, F32),
                vmem(chunks, F32),
                vmem(lines, F32),
                vmem(lines, F32),
                vmem((LEVELS, *lines), F32),
                vmem((LEVELS, *rows), F32),
                vmem(block, F32),
                pltpu.SemaphoreType.DMA((9,)),
                pltpu.SemaphoreType.DMA((PHASES,)),
                pltpu.SemaphoreType.DMA((PHASES,)),
            ],
            compiler_params=pltpu.CompilerParams(collective_id=0, has_side_effects=True),
        )(initial, reaction, *[jnp.asarray(t) for t in constants])

    in_specs = (P("gx", "gy", None), P("gx", "gy", None))
    out_specs = P("lvl", "gx", "gy", None)
    return jax.shard_map(shards, mesh=mesh, in_specs=in_specs, out_specs=out_specs, check_vma=False)
```

time: 297 us -> 84.4 us (0.28)
  the two profiles are of different devices: /device:TPU:1 before, /device:TPU:64 now
where the time goes in v1:
time: 84.4 us; the launch traced here: 84.2 us
  Pallas kernels  82.3 us (98%)
  local copies, waits for them, and re-layouts  1.88 us (2%)
    pallas_call x1, Pallas kernels, shards(): pl.pallas_call(kernel, out_shape=jax.ShapeDtypeStruct((1, *block), F32),...  82.3 us
    unnamed x1, local copies, waits for them, and re-layouts  1.88 us

profile of v1, /device:TPU:64, one launch (start us, length us, event | category | flops | bytes accessed | tf_op | source)
XLA Modules:
  0.0 84.2 jit_solution(12063344973325509688)
XLA Ops:
  0.0 82.3 %shard_map.82 = f32[1,16,32,256]{3,2,1,0:T(8,128)} custom-call(f32[16,32,256]{2,1,0:T(8,128)} %v_hbm.1, f32[16,32,256]{2,1,0:T(8,128)} %r_hbm.1, bf16[512,128]{1,0:T(8,128)(2,1)} %constant.12.clone.tz_hbm, bf16[512,256]{1,0:T(8,128)(2,1)} %constant.13.clone.ty_hbm, bf16[512,256]{1,0:T(8,128)(2,1)} %constant.14.clone.tx_hbm, ...), custom_call_target="tpu_custom_call" | custom-call | tf_op jit(solution)/shard_map/pallas_call | solution.py:413
  82.3 1.9 %copy.10 = f32[1,16,32,256]{3,2,1,0:T(8,128)} copy(f32[1,16,32,256]{3,2,1,0:T(8,128)} %shard_map.82) | data formatting | bytes 1048576

commit v2 on v1

--- a/solution.py
+++ b/solution.py
@@ -17,6 +17,8 @@
 PARTS_Y = 8
 PLANE = LEVELS * PARTS_X
 SLAB = CELLS // PLANE
+PAIRS = PLANE // 2
+LINES_Y = MODES // PAIRS
 ROWS_Y = CELLS // PARTS_Y
 ROWS_X = CELLS // PARTS_X
 RING_Z = 16
@@ -108,56 +110,58 @@
 
 def swap_groups(mats):
     mats = list(mats)
-    group = lane_index(mats[0].shape) // 16
-    for bit in (1, 2, 4):
+    count = len(mats)
+    width = LANES // count
+    group = lane_index(mats[0].shape) // width
+    bit = 1
+    while bit < count:
         keep = (group & bit) == 0
-        for low in range(8):
+        for low in range(count):
             if low & bit:
                 continue
             high = low | bit
             a, b = mats[low], mats[high]
-            mats[low] = jnp.where(keep, a, roll(b, 16 * bit))
-            mats[high] = jnp.where(keep, roll(a, -16 * bit), b)
+            mats[low] = jnp.where(keep, a, roll(b, width * bit))
+            mats[high] = jnp.where(keep, roll(a, -width * bit), b)
+        bit *= 2
     return mats
 
 
+def hops(dy, dz):
+    return min(dy, RING_Y - dy) + min(dz, RING_Z - dz)
+
+
+def offsets():
+    every = [(dy, dz) for dz in range(RING_Z) for dy in range(RING_Y) if (dy, dz) != (0, 0)]
+    every.sort(key=lambda o: -hops(*o))
+    near = []
+    for dy, dz in every:
+        opposite = ((dy + 2) % RING_Y, (dz + 8) % RING_Z)
+        if opposite not in near and hops(dy, dz) <= hops(*opposite):
+            near.append((dy, dz))
+    return every, near
+
+
 def kernel(
-    v_hbm, r_hbm, tz_hbm, ty_hbm, tx_hbm, bx_hbm, by_hbm, bz_hbm, out_hbm,
+    v_hbm, r_hbm, tz_hbm, ty_hbm, tx_hbm, bx_hbm, by_hbm, bz_hbm, piece,
     v, r, r_all, tz, ty, tx, bx, by, bz,
-    factor, carry, y_send, y_recv, x_send, x_recv, b_send, b_recv, u_send, u_recv, f_recv,
-    piece_send, piece, load_sem, send_sem, recv_sem,
+    factor, carry, y_send, y_recv, x_send, x_recv1, x_recv2, b_send, b_recv, u_send, u_recv, f_recv,
+    piece_send, load_sem, send_sem, recv_sem, ready,
 ):
     lvl, gx, gy = lax.axis_index("lvl"), lax.axis_index("gx"), lax.axis_index("gy")
     row_y, high_z = lax.div(gx, 4), lax.rem(gx, 4)
     at_z = high_z * 4 + lvl
     me = row_y * RING_Z + at_z
 
+    pair = lax.rem(row_y, 2) * RING_Z + lax.rem(at_z + 8 * lax.div(row_y, 2), RING_Z)
+
+    def place(dy, dz):
+        return lax.rem(row_y + dy, RING_Y), lax.rem(at_z + dz, RING_Z)
+
     def plane_id(y2, z2):
         return {"gx": y2 * 4 + lax.div(z2, 4), "lvl": lax.rem(z2, 4)}
 
-    def over_plane(do):
-        def body(k, carried):
-            half = lax.div(k + 1, 2)
-            dz = 8 + half * (1 - 2 * lax.rem(k, 2))
-            z2 = lax.rem(at_z + dz, RING_Z)
-            for dy in (2, 1, 3, 0):
-                do(lax.rem(row_y + dy, RING_Y), z2)
-            return carried
-
-        lax.fori_loop(0, RING_Z - 1, body, 0)
-        for dy in (2, 1, 3):
-            do(lax.rem(row_y + dy, RING_Y), at_z)
-
-    barrier = pltpu.get_barrier_semaphore()
-
-    def hello(y2, z2):
-        pl.semaphore_signal(barrier, inc=1, device_id=plane_id(y2, z2), device_id_type=MESH)
-
-    over_plane(hello)
-    for k in range(1, PARTS_Y):
-        pl.semaphore_signal(
-            barrier, inc=1, device_id={"gy": lax.rem(gy + k, PARTS_Y)}, device_id_type=MESH
-        )
+    every, near = offsets()
 
     own = pl.ds(lvl * SLAB, SLAB)
     loads = [
@@ -176,7 +180,23 @@
             ]
         )
     ]
-    for load in loads:
+    for load in loads[:3]:
+        load.start()
+
+    barrier = pltpu.get_barrier_semaphore()
+    heard = 0
+    for dy, dz in every:
+        if min(dz, RING_Z - dz) <= 4:
+            pl.semaphore_signal(
+                barrier, inc=1, device_id=plane_id(*place(dy, dz)), device_id_type=MESH
+            )
+            heard += 1
+    for k in (4, 3, 5, 2, 6, 1, 7):
+        pl.semaphore_signal(
+            barrier, inc=1, device_id={"gy": lax.rem(gy + k, PARTS_Y)}, device_id_type=MESH
+        )
+        heard += 1
+    for load in loads[3:]:
         load.start()
 
     def remote(source, target, phase, device_id, send_phase=None):
@@ -201,20 +221,28 @@
             remote(source.at[other], target.at[gy], phase, {"gy": other}).start()
         target[gy] = source[gy]
 
-    def x_exchange(source, target, phase, shift):
+    def x_exchange(x_recv, phase):
+        def send(y2, z2):
+            chunk = lax.rem(y2, 2) * RING_Z + lax.rem(z2 + 8 * lax.div(y2, 2), RING_Z)
+            remote(x_send.at[chunk], x_recv.at[me], phase, plane_id(y2, z2)).start()
+
+        for dy, dz in every:
+            send(*place(dy, dz))
+        x_recv[me] = x_send[pair]
+
+    def x_return(phase, shift):
         def chunk_of(y2, z2):
             return y2 * RING_Z + lax.rem(z2 + RING_Z - shift, RING_Z)
 
-        def send(y2, z2):
-            remote(source.at[chunk_of(y2, z2)], target.at[me], phase, plane_id(y2, z2)).start()
-
-        over_plane(send)
-        target[me] = source[chunk_of(row_y, at_z)]
+        for dy, dz in near:
+            y2, z2 = place(dy, dz)
+            remote(b_send.at[chunk_of(y2, z2)], b_recv.at[pair], phase, plane_id(y2, z2)).start()
+        b_recv[pair] = b_send[chunk_of(row_y, at_z)]
 
     shape = (MODES, LANES)
     lane = lane_index(shape)
     wave_x = (lax.broadcasted_iota(jnp.int32, shape, 0) - MODES // 2).astype(F32) / (CELLS // 4)
-    wave_y = ((lane // 32 & 1) + 2 * me - MODES // 2).astype(F32) / (CELLS // 4)
+    wave_y = (lane // 32 + LINES_Y * pair - MODES // 2).astype(F32) / (CELLS // 4)
     wave_z = ((lane & 7) + 8 * gy).astype(F32) / (CELLS // 4)
     factor[0] = -DIFFUSE * (wave_x * wave_x + wave_y * wave_y + wave_z * wave_z) * NORM
     factor[1] = -(0.3 * wave_x + 0.2 * wave_y + 0.25 * wave_z) * NORM
@@ -246,18 +274,10 @@
         lines = both[:MODES] - turn(both[MODES:])
         x_send.reshape(MODES, LANES)[...] = lines
 
-    def x_middle(carried):
-        rows = x_recv.reshape(MODES, LANES)
-        first = rows[pl.ds(0, PLANE, stride=2), :]
-        second = rows[pl.ds(1, PLANE, stride=2), :]
-        low = lane_index(first.shape) < 32
-        lines = jnp.concatenate(
-            [
-                jnp.where(low, roll(first, -32 * i), roll(second, 32 - 32 * i))
-                for i in range(SLAB)
-            ],
-            axis=0,
-        )
+    def x_middle(x_recv, carried):
+        rows = x_recv.reshape(CELLS, LANES)
+        mats = [rows[pl.ds(ky, PLANE, stride=LINES_Y), :] for ky in range(LINES_Y)]
+        lines = jnp.concatenate(swap_groups(mats), axis=0)
         both = table_times(tx, lines)
         spectrum = both[:MODES] - turn(both[MODES:])
         is_first = (lane & 16) == 0
@@ -268,14 +288,10 @@
         if not carried:
             carry[...] = rate
         lines = table_times(bx, jnp.concatenate([rate, turn(rate)], axis=0))
-        group = lane_index((PLANE, LANES)) // 32
-        target = b_send.reshape(MODES, LANES)
-        for ky in range(2):
-            out = None
-            for i in range(SLAB):
-                piece_i = roll(lines[i * PLANE : (i + 1) * PLANE], 32 * (i - ky))
-                out = piece_i if out is None else jnp.where(group == i, piece_i, out)
-            target[pl.ds(ky, PLANE, stride=2), :] = out
+        target = b_send.reshape(CELLS, LANES)
+        mats = [lines[i * PLANE : (i + 1) * PLANE] for i in range(SLAB)]
+        for ky, mat in enumerate(swap_groups(mats)):
+            target[pl.ds(ky, PLANE, stride=LINES_Y), :] = mat
 
     def y_back():
         lines = b_recv.reshape(MODES, LANES)[...]
@@ -289,18 +305,22 @@
     z_forward(start, react * start)
     for i in range(3, 8):
         loads[i].wait()
-    pl.semaphore_wait(barrier, PLANE - 1 + PARTS_Y - 1)
+    pl.semaphore_wait(barrier, heard)
+    for dz in (4, RING_Z - 4):
+        pl.semaphore_signal(ready, inc=1, device_id=plane_id(*place(0, dz)), device_id_type=MESH)
 
     others_y = pl.ds(0, PARTS_Y - 1)
     others_x = pl.ds(0, PLANE - 1)
+    others_b = pl.ds(0, PAIRS - 1)
     y_exchange(y_send, y_recv, Y_OUT)
     received(y_recv.at[others_y], Y_OUT)
     y_forward()
-    x_exchange(x_send, x_recv, X_OUT, 0)
-    received(x_recv.at[others_x], X_OUT)
-    x_middle(False)
-    x_exchange(b_send, b_recv, X_BACK, 0)
-    received(b_recv.at[others_x], X_BACK)
+    pl.semaphore_wait(ready, 2)
+    x_exchange(x_recv1, X_OUT)
+    received(x_recv1.at[others_x], X_OUT)
+    x_middle(x_recv1, False)
+    x_return(X_BACK, 0)
+    received(b_recv.at[others_b], X_BACK)
     y_back()
     sent(y_send.at[others_y], Y_OUT)
     y_exchange(u_send, u_recv, Y_BACK)
@@ -310,8 +330,8 @@
     rate2 = smooth_rate + react * rate1
     z_forward(react * rate1, react * rate2)
 
-    sent(x_send.at[others_x], X_OUT)
-    sent(b_send.at[others_x], X_BACK)
+    sent(x_recv1.at[others_x], X_OUT)
+    sent(b_send.at[others_b], X_BACK)
     y_exchange(y_send, y_recv, Y_OUT2)
     known = start + rate1
     piece_send[0] = known.reshape(SLAB, ROWS_Y, CELLS)
@@ -321,18 +341,27 @@
     piece_send[2] = known.reshape(SLAB, ROWS_Y, CELLS)
     known = known + 0.125 * (react * (react * rate2))
     piece_send[3] = known.reshape(SLAB, ROWS_Y, CELLS)
-    for k in range(1, LEVELS):
-        other = lax.rem(lvl + k, LEVELS)
-        remote(piece_send.at[other], piece.at[own], BULK, {"lvl": other}).start()
+
+    def send_pieces(first, last):
+        for row in range(first, last):
+            for k in range(1, LEVELS):
+                other = lax.rem(lvl + k, LEVELS)
+                target = piece.at[lvl * SLAB + row]
+                remote(piece_send.at[other, row], target, BULK, {"lvl": other}).start()
+
+    send_pieces(0, 1)
     piece[own] = piece_send[lvl]
 
     received(y_recv.at[others_y], Y_OUT2)
     y_forward()
-    x_exchange(x_send, x_recv, X_OUT2, 0)
-    received(x_recv.at[others_x], X_OUT2)
-    x_middle(True)
-    x_exchange(b_send, b_recv, X_BACK2, 1)
-    received(b_recv.at[others_x], X_BACK2)
+    x_exchange(x_recv2, X_OUT2)
+    send_pieces(1, 2)
+    received(x_recv2.at[others_x], X_OUT2)
+    send_pieces(2, 3)
+    x_middle(x_recv2, True)
+    x_return(X_BACK2, 1)
+    send_pieces(3, 4)
+    received(b_recv.at[others_b], X_BACK2)
     sent(u_send.at[others_y], Y_BACK)
     y_back()
 
@@ -382,12 +411,10 @@
             second = second.reshape(SLAB, ROWS_Y, CELLS)
             piece[at] = piece[at] + (0.25 + last_weight * r_all[at]) * first + last_weight * second
 
-    result = pltpu.make_async_copy(piece, out_hbm.at[0], load_sem.at[0])
-    result.start()
 
     sent(y_send.at[others_y], Y_OUT2)
-    sent(x_send.at[others_x], X_OUT2)
-    sent(b_send.at[others_x], X_BACK2)
+    sent(x_recv2.at[others_x], X_OUT2)
+    sent(b_send.at[others_b], X_BACK2)
     sent(piece_send.at[pl.ds(0, 3)], BULK)
     for level in (3, 2):
         @pl.when(lvl != level)
@@ -398,8 +425,6 @@
         def _(level=level):
             sent(u_send.at[others_y], FINAL + level)
 
-    result.wait()
-
 
 def solution(mesh):
     constants = tables()
@@ -408,13 +433,14 @@
         rows = (SLAB, ROWS_Y, CELLS)
         block = (ROWS_X, ROWS_Y, CELLS)
         lines = (PARTS_Y, ROWS_Y, LANES)
-        chunks = (PLANE, 2, LANES)
+        chunks = (PLANE, LINES_Y, LANES)
+        half_chunks = (PAIRS, LINES_Y, LANES)
         vmem = pltpu.VMEM
-        return pl.pallas_call(
+        result = pl.pallas_call(
             kernel,
-            out_shape=jax.ShapeDtypeStruct((1, *block), F32),
+            out_shape=pltpu.VMEM(block, F32),
             in_specs=[pl.BlockSpec(memory_space=pl.ANY)] * 8,
-            out_specs=pl.BlockSpec(memory_space=pl.ANY),
+            out_specs=pl.BlockSpec(memory_space=pltpu.VMEM),
             scratch_shapes=[
                 vmem(rows, F32),
                 vmem(rows, F32),
@@ -424,21 +450,23 @@
                 vmem((MODES, LANES), F32),
                 vmem(lines, F32),
                 vmem(lines, F32),
+                vmem(half_chunks, F32),
                 vmem(chunks, F32),
                 vmem(chunks, F32),
                 vmem(chunks, F32),
-                vmem(chunks, F32),
+                vmem(half_chunks, F32),
                 vmem(lines, F32),
                 vmem(lines, F32),
                 vmem((LEVELS, *lines), F32),
                 vmem((LEVELS, *rows), F32),
-                vmem(block, F32),
                 pltpu.SemaphoreType.DMA((9,)),
                 pltpu.SemaphoreType.DMA((PHASES,)),
                 pltpu.SemaphoreType.DMA((PHASES,)),
+                pltpu.SemaphoreType.REGULAR,
             ],
             compiler_params=pltpu.CompilerParams(collective_id=0, has_side_effects=True),
         )(initial, reaction, *[jnp.asarray(t) for t in constants])
+        return result[None]
 
     in_specs = (P("gx", "gy", None), P("gx", "gy", None))
     out_specs = P("lvl", "gx", "gy", None)

time: 84.4 us -> 73 us (0.86)
  Pallas kernels: 82.3 us -> 71.6 us
  local copies, waits for them, and re-layouts: 1.88 us -> 0.8 us
    pallas_call x1, Pallas kernels: 82.3 us -> 71.6 us  [shards(): pl.pallas_call(kernel, out_shape=pltpu.VMEM(block, F32), in_specs=[pl.Blo...]
    unnamed x1, local copies, waits for them, and re-layouts: 1.88 us -> 0.8 us
where the time goes in v2:
time: 73 us; the launch traced here: 72.4 us
  Pallas kernels  71.6 us (98%)
  local copies, waits for them, and re-layouts  0.8 us (1%)
    pallas_call x1, Pallas kernels, shards(): pl.pallas_call(kernel, out_shape=pltpu.VMEM(block, F32), in_specs=[pl.Blo...  71.6 us

profile of v2, /device:TPU:64, one launch (start us, length us, event | category | flops | bytes accessed | tf_op | source)
XLA Modules:
  0.0 72.4 jit_solution(18309201831788165819)
XLA Ops:
  0.0 71.6 %shard_map.82 = f32[16,32,256]{2,1,0:T(8,128)S(1)} custom-call(f32[16,32,256]{2,1,0:T(8,128)} %v_hbm.1, f32[16,32,256]{2,1,0:T(8,128)} %r_hbm.1, bf16[512,128]{1,0:T(8,128)(2,1)} %constant.12.clone.tz_hbm, bf16[512,256]{1,0:T(8,128)(2,1)} %constant.13.clone.ty_hbm, bf16[512,256]{1,0:T(8,128)(2,1)} %constant.14.clone.tx_hbm, ...), custom_call_target="tpu_custom_call" | custom-call | tf_op jit(solution)/shard_map/pallas_call | solution.py:439
  71.6 0.8 %copy.10 = f32[1,16,32,256]{3,2,1,0:T(8,128)} copy(f32[1,16,32,256]{3,2,1,0:T(8,128)S(1)} %bitcast.1) | data formatting | bytes 1048576

commit v3 on v2

--- a/solution.py
+++ b/solution.py
@@ -32,6 +32,7 @@
 
 Y_OUT, X_OUT, X_BACK, Y_BACK, Y_OUT2, X_OUT2, X_BACK2, BULK, FINAL = range(9)
 PHASES = FINAL + LEVELS
+CUTS = ((1, 2, 5, 8), (2, 4, 8, 8))
 
 
 def halves(table):
@@ -186,7 +187,7 @@
     barrier = pltpu.get_barrier_semaphore()
     heard = 0
     for dy, dz in every:
-        if min(dz, RING_Z - dz) <= 4:
+        if min(dz, RING_Z - dz) <= 4 and dy != 2:
             pl.semaphore_signal(
                 barrier, inc=1, device_id=plane_id(*place(dy, dz)), device_id_type=MESH
             )
@@ -239,18 +240,16 @@
             remote(b_send.at[chunk_of(y2, z2)], b_recv.at[pair], phase, plane_id(y2, z2)).start()
         b_recv[pair] = b_send[chunk_of(row_y, at_z)]
 
-    shape = (MODES, LANES)
-    lane = lane_index(shape)
-    wave_x = (lax.broadcasted_iota(jnp.int32, shape, 0) - MODES // 2).astype(F32) / (CELLS // 4)
-    wave_y = (lane // 32 + LINES_Y * pair - MODES // 2).astype(F32) / (CELLS // 4)
-    wave_z = ((lane & 7) + 8 * gy).astype(F32) / (CELLS // 4)
-    factor[0] = -DIFFUSE * (wave_x * wave_x + wave_y * wave_y + wave_z * wave_z) * NORM
-    factor[1] = -(0.3 * wave_x + 0.2 * wave_y + 0.25 * wave_z) * NORM
-    edge = (wave_z == 0.0) & ((wave_x == -1.0) | (wave_y == -1.0))
-    factor[2] = jnp.where(edge, 0.5 / NORM, 1.0 / NORM)
-
-    def scaled(x):
-        return factor[0] * x + factor[1] * turn(x)
+    def prepare_factor():
+        shape = (MODES, LANES)
+        lane = lane_index(shape)
+        wave_x = (lax.broadcasted_iota(jnp.int32, shape, 0) - MODES // 2).astype(F32) / (CELLS // 4)
+        wave_y = (lane // 32 + LINES_Y * pair - MODES // 2).astype(F32) / (CELLS // 4)
+        wave_z = ((lane & 7) + 8 * gy).astype(F32) / (CELLS // 4)
+        factor[0] = -DIFFUSE * (wave_x * wave_x + wave_y * wave_y + wave_z * wave_z) * NORM
+        factor[1] = -(0.3 * wave_x + 0.2 * wave_y + 0.25 * wave_z) * NORM
+        edge = (wave_z == 0.0) & ((wave_x == -1.0) | (wave_y == -1.0))
+        factor[2] = jnp.where(edge, 0.5 / NORM, 1.0 / NORM)
 
     def z_forward(first, second):
         lines = times_table(jnp.concatenate([first, second], axis=0), tz)
@@ -279,19 +278,31 @@
         mats = [rows[pl.ds(ky, PLANE, stride=LINES_Y), :] for ky in range(LINES_Y)]
         lines = jnp.concatenate(swap_groups(mats), axis=0)
         both = table_times(tx, lines)
-        spectrum = both[:MODES] - turn(both[MODES:])
-        is_first = (lane & 16) == 0
+        cosine, sine = both[:MODES], both[MODES:]
+        real, imag = factor[0], factor[1]
+        first = (lane_index(cosine.shape) & 16) == 0
+        spectrum, turned = cosine - turn(sine), turn(cosine) + sine
         if carried:
-            spectrum = spectrum + jnp.where(is_first, roll(factor[2] * carry[...], -16), 0.0)
-        rate = scaled(spectrum)
-        rate = jnp.where(is_first, rate, scaled(roll(factor[2] * rate, 16) + spectrum))
+            spectrum, turned = spectrum + carry[0], turned + carry[1]
+        rate = real * spectrum + imag * turned
+        rate_turned = real * turned - imag * spectrum
+        spectrum = factor[2] * roll(rate, 16) + spectrum
+        turned = factor[2] * roll(rate_turned, 16) + turned
+        rate = jnp.where(first, rate, real * spectrum + imag * turned)
+        rate_turned = jnp.where(first, rate_turned, real * turned - imag * spectrum)
         if not carried:
-            carry[...] = rate
-        lines = table_times(bx, jnp.concatenate([rate, turn(rate)], axis=0))
+            carry[0] = rate
+            carry[1] = rate_turned
+        lines = table_times(bx, jnp.concatenate([rate, rate_turned], axis=0))
         target = b_send.reshape(CELLS, LANES)
         mats = [lines[i * PLANE : (i + 1) * PLANE] for i in range(SLAB)]
         for ky, mat in enumerate(swap_groups(mats)):
             target[pl.ds(ky, PLANE, stride=LINES_Y), :] = mat
+
+    def prepare_carry():
+        first = (lane_index((MODES, LANES)) & 16) == 0
+        for i in range(2):
+            carry[i] = jnp.where(first, factor[2] * roll(carry[i], -16), 0.0)
 
     def y_back():
         lines = b_recv.reshape(MODES, LANES)[...]
@@ -306,20 +317,25 @@
     for i in range(3, 8):
         loads[i].wait()
     pl.semaphore_wait(barrier, heard)
-    for dz in (4, RING_Z - 4):
-        pl.semaphore_signal(ready, inc=1, device_id=plane_id(*place(0, dz)), device_id_type=MESH)
+    for dy in (3, 0):
+        for dz in (4, RING_Z - 4):
+            pl.semaphore_signal(
+                ready, inc=1, device_id=plane_id(*place(dy, dz)), device_id_type=MESH
+            )
 
     others_y = pl.ds(0, PARTS_Y - 1)
     others_x = pl.ds(0, PLANE - 1)
     others_b = pl.ds(0, PAIRS - 1)
     y_exchange(y_send, y_recv, Y_OUT)
+    prepare_factor()
     received(y_recv.at[others_y], Y_OUT)
     y_forward()
-    pl.semaphore_wait(ready, 2)
+    pl.semaphore_wait(ready, 4)
     x_exchange(x_recv1, X_OUT)
     received(x_recv1.at[others_x], X_OUT)
     x_middle(x_recv1, False)
     x_return(X_BACK, 0)
+    prepare_carry()
     received(b_recv.at[others_b], X_BACK)
     y_back()
     sent(y_send.at[others_y], Y_OUT)
@@ -342,25 +358,29 @@
     known = known + 0.125 * (react * (react * rate2))
     piece_send[3] = known.reshape(SLAB, ROWS_Y, CELLS)
 
-    def send_pieces(first, last):
-        for row in range(first, last):
-            for k in range(1, LEVELS):
-                other = lax.rem(lvl + k, LEVELS)
-                target = piece.at[lvl * SLAB + row]
-                remote(piece_send.at[other, row], target, BULK, {"lvl": other}).start()
-
-    send_pieces(0, 1)
+    def send_pieces(point):
+        for level in range(LEVELS):
+            cuts = (0, *CUTS[level // 2])
+
+            @pl.when(lvl != level)
+            def _(level=level, cuts=cuts):
+                for at in range(cuts[point], cuts[point + 1]):
+                    half = pl.ds(at % 2 * (ROWS_Y // 2), ROWS_Y // 2)
+                    source = piece_send.at[level, at // 2, half]
+                    target = piece.at[lvl * SLAB + at // 2, half]
+                    remote(source, target, BULK, {"lvl": level}).start()
+
+    send_pieces(0)
     piece[own] = piece_send[lvl]
 
     received(y_recv.at[others_y], Y_OUT2)
     y_forward()
     x_exchange(x_recv2, X_OUT2)
-    send_pieces(1, 2)
+    send_pieces(1)
     received(x_recv2.at[others_x], X_OUT2)
-    send_pieces(2, 3)
     x_middle(x_recv2, True)
     x_return(X_BACK2, 1)
-    send_pieces(3, 4)
+    send_pieces(2)
     received(b_recv.at[others_b], X_BACK2)
     sent(u_send.at[others_y], Y_BACK)
     y_back()
@@ -390,21 +410,19 @@
         def _():
             f_recv[slab, gy] = u_send[gy]
 
+    send_pieces(3)
     loads[8].wait()
     received(piece.at[pl.ds(0, ROWS_X - SLAB)], BULK)
 
     @pl.when(lvl >= 2)
     def _():
         last_weight = jnp.where(lvl == 3, 0.125, 0.0)
-        for t in range(LEVELS):
-            @pl.when(lvl - 1 != t)
-            def _(t=t):
+        for step in (0, 3, 1, 2):
+            t = lax.rem(lvl - 1 + step, LEVELS)
+            if step == 0:
+                received(f_recv.at[t, others_y], FINAL + t)
+            else:
                 received(f_recv.at[t], FINAL + t)
-
-            @pl.when(lvl - 1 == t)
-            def _(t=t):
-                received(f_recv.at[t, others_y], FINAL + t)
-
             first, second = z_back([f_recv[t, part] for part in range(PARTS_Y)])
             at = pl.ds(t * SLAB, SLAB)
             first = first.reshape(SLAB, ROWS_Y, CELLS)
@@ -447,7 +465,7 @@
                 vmem(block, F32),
                 *[vmem(t.shape, BF16) for t in constants],
                 vmem((3, MODES, LANES), F32),
-                vmem((MODES, LANES), F32),
+                vmem((2, MODES, LANES), F32),
                 vmem(lines, F32),
                 vmem(lines, F32),
                 vmem(half_chunks, F32),

time: 73 us -> 70.4 us (0.964)
  the two profiles are of different devices: /device:TPU:64 before, /device:TPU:4 now
where the time goes in v3:
time: 70.4 us; the launch traced here: 70.2 us
  Pallas kernels  69.4 us (99%)
  local copies, waits for them, and re-layouts  0.8 us (1%)
    pallas_call x1, Pallas kernels, shards(): pl.pallas_call(kernel, out_shape=pltpu.VMEM(block, F32), in_specs=[pl.Blo...  69.4 us

profile of v3, /device:TPU:4, one launch (start us, length us, event | category | flops | bytes accessed | tf_op | source)
XLA Modules:
  0.0 70.2 jit_solution(11906689388808678925)
XLA Ops:
  0.0 69.4 %shard_map.82 = f32[16,32,256]{2,1,0:T(8,128)S(1)} custom-call(f32[16,32,256]{2,1,0:T(8,128)} %v_hbm.1, f32[16,32,256]{2,1,0:T(8,128)} %r_hbm.1, bf16[512,128]{1,0:T(8,128)(2,1)} %constant.12.clone.tz_hbm, bf16[512,256]{1,0:T(8,128)(2,1)} %constant.13.clone.ty_hbm, bf16[512,256]{1,0:T(8,128)(2,1)} %constant.14.clone.tx_hbm, ...), custom_call_target="tpu_custom_call" | custom-call | tf_op jit(solution)/shard_map/pallas_call | solution.py:457
  69.4 0.8 %copy.10 = f32[1,16,32,256]{3,2,1,0:T(8,128)} copy(f32[1,16,32,256]{3,2,1,0:T(8,128)S(1)} %bitcast.1) | data formatting | bytes 1048576

commit v4 on v3

--- a/solution.py
+++ b/solution.py
@@ -32,7 +32,7 @@
 
 Y_OUT, X_OUT, X_BACK, Y_BACK, Y_OUT2, X_OUT2, X_BACK2, BULK, FINAL = range(9)
 PHASES = FINAL + LEVELS
-CUTS = ((1, 2, 5, 8), (2, 4, 8, 8))
+CUTS = ((1, 2, 6, 8), (2, 4, 8, 8))
 
 
 def halves(table):
@@ -417,18 +417,20 @@
     @pl.when(lvl >= 2)
     def _():
         last_weight = jnp.where(lvl == 3, 0.125, 0.0)
-        for step in (0, 3, 1, 2):
-            t = lax.rem(lvl - 1 + step, LEVELS)
-            if step == 0:
-                received(f_recv.at[t, others_y], FINAL + t)
-            else:
-                received(f_recv.at[t], FINAL + t)
-            first, second = z_back([f_recv[t, part] for part in range(PARTS_Y)])
-            at = pl.ds(t * SLAB, SLAB)
-            first = first.reshape(SLAB, ROWS_Y, CELLS)
-            second = second.reshape(SLAB, ROWS_Y, CELLS)
-            piece[at] = piece[at] + (0.25 + last_weight * r_all[at]) * first + last_weight * second
-
+        def add(steps):
+            slabs = [lax.rem(lvl - 1 + step, LEVELS) for step in steps]
+            for t, step in zip(slabs, steps):
+                received(f_recv.at[t] if step else f_recv.at[t, others_y], FINAL + t)
+            parts = [z_back([f_recv[t, part] for part in range(PARTS_Y)]) for t in slabs]
+            for t, (first, second) in zip(slabs, parts):
+                at = pl.ds(t * SLAB, SLAB)
+                first = first.reshape(SLAB, ROWS_Y, CELLS)
+                second = second.reshape(SLAB, ROWS_Y, CELLS)
+                scale = 0.25 + last_weight * r_all[at]
+                piece[at] = piece[at] + scale * first + last_weight * second
+
+        add((0,))
+        add((3, 1, 2))
 
     sent(y_send.at[others_y], Y_OUT2)
     sent(x_recv2.at[others_x], X_OUT2)

time: 70.4 us -> 69.9 us (level)
  the two profiles are of different devices: /device:TPU:4 before, /device:TPU:64 now
where the time goes in v4:
time: 69.9 us; the launch traced here: 69.8 us
  Pallas kernels  69 us (99%)
  local copies, waits for them, and re-layouts  0.8 us (1%)
    pallas_call x1, Pallas kernels, shards(): pl.pallas_call(kernel, out_shape=pltpu.VMEM(block, F32), in_specs=[pl.Blo...  69 us

profile of v4, /device:TPU:64, one launch (start us, length us, event | category | flops | bytes accessed | tf_op | source)
XLA Modules:
  0.0 69.8 jit_solution(3412591650614078236)
XLA Ops:
  0.0 69.0 %shard_map.82 = f32[16,32,256]{2,1,0:T(8,128)S(1)} custom-call(f32[16,32,256]{2,1,0:T(8,128)} %v_hbm.1, f32[16,32,256]{2,1,0:T(8,128)} %r_hbm.1, bf16[512,128]{1,0:T(8,128)(2,1)} %constant.12.clone.tz_hbm, bf16[512,256]{1,0:T(8,128)(2,1)} %constant.13.clone.ty_hbm, bf16[512,256]{1,0:T(8,128)(2,1)} %constant.14.clone.tx_hbm, ...), custom_call_target="tpu_custom_call" | custom-call | tf_op jit(solution)/shard_map/pallas_call | solution.py:459
  69.0 0.8 %copy.10 = f32[1,16,32,256]{3,2,1,0:T(8,128)} copy(f32[1,16,32,256]{3,2,1,0:T(8,128)S(1)} %bitcast.1) | data formatting | bytes 1048576

commit v5 on v4

--- a/solution.py
+++ b/solution.py
@@ -32,7 +32,7 @@
 
 Y_OUT, X_OUT, X_BACK, Y_BACK, Y_OUT2, X_OUT2, X_BACK2, BULK, FINAL = range(9)
 PHASES = FINAL + LEVELS
-CUTS = ((1, 2, 6, 8), (2, 4, 8, 8))
+CUTS = ((1, 3, 7, 8), (2, 4, 8, 8))
 
 
 def halves(table):

time: 69.9 us -> 70.4 us (level)
  the two profiles are of different devices: /device:TPU:64 before, /device:TPU:2 now
where the time goes in v5:
time: 70.4 us; the launch traced here: 70.2 us
  Pallas kernels  69.4 us (99%)
  local copies, waits for them, and re-layouts  0.8 us (1%)
    pallas_call x1, Pallas kernels, shards(): pl.pallas_call(kernel, out_shape=pltpu.VMEM(block, F32), in_specs=[pl.Blo...  69.4 us

profile of v5, /device:TPU:2, one launch (start us, length us, event | category | flops | bytes accessed | tf_op | source)
XLA Modules:
  0.0 70.2 jit_solution(13646233010850658109)
XLA Ops:
  0.0 69.4 %shard_map.82 = f32[16,32,256]{2,1,0:T(8,128)S(1)} custom-call(f32[16,32,256]{2,1,0:T(8,128)} %v_hbm.1, f32[16,32,256]{2,1,0:T(8,128)} %r_hbm.1, bf16[512,128]{1,0:T(8,128)(2,1)} %constant.12.clone.tz_hbm, bf16[512,256]{1,0:T(8,128)(2,1)} %constant.13.clone.ty_hbm, bf16[512,256]{1,0:T(8,128)(2,1)} %constant.14.clone.tx_hbm, ...), custom_call_target="tpu_custom_call" | custom-call | tf_op jit(solution)/shard_map/pallas_call | solution.py:459
  69.4 0.8 %copy.10 = f32[1,16,32,256]{3,2,1,0:T(8,128)} copy(f32[1,16,32,256]{3,2,1,0:T(8,128)S(1)} %bitcast.1) | data formatting | bytes 1048576
